TPU v7x, 32 devices: a whole 2x2x4 slice. The times are simulated.
32 devices in a mesh: pw: 16 (over z, x, core), ka: 2 (over y).
Axes of the slice: x: 2, y: 2, z: 4, core: 2. Of those that a mesh axis runs over, the one named last changes fastest.
Arguments:
- waves: bfloat16 [2, 2, 32768, 256], P('ka', None, 'pw'), may hold values from -0.125 to 0.125
- projectors: bfloat16 [2, 2, 32768, 2304], P('ka', None, 'pw'), may hold values from -0.125 to 0.125
- projector_order: int32 [2304], replicated, may hold values from 0 to 2303, each once
- shift_map: int32 [32768], P('pw'), may hold values from 0 to 32767, as said below
- charges: float32 [128, 18, 18], replicated, may hold values from -0.125 to 0.125
- atom_phase: float32 [128], replicated, may hold values from -3.140625 to 3.140625
Outputs:
- margins: float32 [2, 256, 2, 256], P('ka', 'pw')
Inputs may be any that keep to these rules, and one draw needn't show every extreme that they name: `projector_order`: each projector slot once. `shift_map`: a permutation of the plane waves that maps every aligned block of 2048 plane waves onto itself.
All inputs are finite; a program needn't handle non-finite values.
Results may differ from a plain program's by a relative error of at most 0.0003.
Values may be sent and summed in bfloat16 or wider, within the bound.
A program may use at most 128 MiB of HBM per device.

v0:
```python
import functools

import jax
import jax.numpy as jnp
from jax import lax
from jax.experimental import pallas as pl
from jax.experimental.pallas import tpu as pltpu
from jax.sharding import PartitionSpec as P

PPA = 18
MESH = pl.DeviceIdType.MESH


def contract(left, right, precision=None):
    return lax.dot_general(
        left,
        right,
        (((0,), (0,)), ((), ())),
        precision=precision,
        preferred_element_type=jnp.float32,
    )


def orders_of(n):
    bits = n.bit_length() - 1
    first = list(range(bits))
    second = [0] + list(range(2, bits)) + [1] if bits > 2 else first
    return first, second


def expand(me, done, free, count):
    index = me & sum(1 << bit for bit in done)
    for place, bit in enumerate(free):
        index = index | (((count >> place) & 1) << bit)
    return index


def halving(n, me, orders, acc, sends, recvs, send_scales, recv_scales, sems):
    bits = len(orders[0])
    rows = acc.shape[2]

    def copies(stream, stage):
        size = n >> (stage + 1)
        base = n - (n >> stage)
        bit = orders[stream][stage]
        partner = me ^ (1 << bit)
        made = []
        for kind, (src, dst) in enumerate(((sends, recvs), (send_scales, recv_scales))):
            made.append(
                pltpu.make_async_remote_copy(
                    src_ref=src.at[stream, pl.ds(base, size)],
                    dst_ref=dst.at[stream, pl.ds(base, size)],
                    send_sem=sems.at[0, stream, stage, kind],
                    recv_sem=sems.at[1, stream, stage, kind],
                    device_id={"pw": partner},
                    device_id_type=MESH,
                )
            )
        return made

    def push(stream, stage):
        size = n >> (stage + 1)
        base = n - (n >> stage)
        bit = orders[stream][stage]
        done = orders[stream][:stage]
        free = [b for b in orders[stream][stage + 1 :]]
        partner = me ^ (1 << bit)

        def code(count, carry):
            chunk = expand(partner, done + [bit], free, count)
            x = acc[stream, chunk]
            top = jnp.max(jnp.abs(x), axis=0, keepdims=True)
            scale = jnp.maximum(top, 1e-30) * (1.0 / 32767.0)
            q = jnp.floor(x * (1.0 / scale) + 0.5)
            sends[stream, base + count] = q.astype(jnp.int32).astype(jnp.int16)
            send_scales[stream, base + count] = scale
            return carry

        lax.fori_loop(0, size, code, 0)
        for copy in copies(stream, stage):
            copy.start()

    def pull(stream, stage):
        size = n >> (stage + 1)
        base = n - (n >> stage)
        bit = orders[stream][stage]
        done = orders[stream][:stage]
        free = [b for b in orders[stream][stage + 1 :]]
        for copy in copies(stream, stage):
            copy.wait()

        def add(count, carry):
            chunk = expand(me, done + [bit], free, count)
            q = recvs[stream, base + count].astype(jnp.int32).astype(jnp.float32)
            acc[stream, chunk] = acc[stream, chunk] + q * recv_scales[stream, base + count]
            return carry

        lax.fori_loop(0, size, add, 0)

    return push, pull, bits


def fused_kernel(
    n, kn, inverse, shift, cosine, sine, sym, wave_hbm, beta_hbm, out,
    wave, beta, rhs, proj, received, own, mine, nextb, kept, local_sems, ka_sems, *scratch
):
    me = lax.axis_index("pw")
    k = lax.axis_index("ka")
    ahead, behind = lax.rem(k + 1, kn), lax.rem(k + kn - 1, kn)
    acc, first = scratch[0], scratch[:6]
    last = scratch[6:]
    acc_last = last[0]
    pw_dev, nb = wave.shape[1], wave.shape[2]
    half = nb // 2
    rows = acc.shape[2]
    tiles = local_sems.shape[0] - 1
    tile = beta.shape[2] // tiles

    def beta_copy(t):
        at = pl.ds(pl.multiple_of(t * tile, tile), tile)
        return pltpu.make_async_copy(beta_hbm.at[0, :, :, at], beta.at[:, :, at], local_sems.at[t + 1])

    own_copy = pltpu.make_async_copy(wave_hbm.at[0], wave, local_sems.at[0])
    own_copy.start()
    for t in range(tiles):
        beta_copy(t).start()

    barrier = pltpu.get_barrier_semaphore()
    bits = n.bit_length() - 1
    for bit in range(bits):
        pl.semaphore_signal(barrier, inc=1, device_id={"pw": me ^ (1 << bit)}, device_id_type=MESH)
    for other in (ahead, behind):
        pl.semaphore_signal(barrier, inc=1, device_id={"ka": other}, device_id_type=MESH)
    pl.semaphore_wait(barrier, bits + 2)

    def ka_copy(src, dst, at):
        return pltpu.make_async_remote_copy(
            src_ref=src,
            dst_ref=dst,
            send_sem=ka_sems.at[0, at],
            recv_sem=ka_sems.at[1, at],
            device_id={"ka": behind},
            device_id_type=MESH,
        )

    wave_copy = ka_copy(wave_hbm.at[0], received, 0)
    wave_copy.start()
    own_copy.wait()
    for stream in range(2):
        cols = slice(stream * half, (stream + 1) * half)
        rhs[stream, 0, :, :half] = wave[0, :, cols]
        rhs[stream, 0, :, half:] = wave[1, :, cols]
        rhs[stream, 1, :, :half] = wave[1, :, cols]
        rhs[stream, 1, :, half:] = -wave[0, :, cols]

    push, pull, bits = halving(n, me, (orders_of(n)[0],) * 2, *first)

    def multiply(stream, low, high):
        def step(t, carry):
            if stream == 0:
                beta_copy(t).wait()
            at = pl.ds(pl.multiple_of(t * tile, tile), tile)
            proj[stream, at, :] = contract(beta[0, :, at], rhs[stream, 0]) + contract(beta[1, :, at], rhs[stream, 1])
            return carry

        lax.fori_loop(low, high, step, 0)

    unit = 48 if rows % 48 == 0 else 16 if rows % 16 == 0 else 1

    def gather(stream, core):
        def one(count, carry):
            chunk = (count << 1) | core

            def some(group, inner):
                low = pl.multiple_of(group * unit, unit)
                ats = [inverse[chunk * rows + low + r] for r in range(unit)]
                taken = [proj[stream, pl.ds(at, 1), :] for at in ats]
                acc[stream, chunk, pl.ds(low, unit), :] = jnp.concatenate(taken, axis=0)
                return inner

            lax.fori_loop(0, rows // unit, some, 0)
            return carry

        lax.fori_loop(0, n // 2, one, 0)

    every = lax.broadcasted_iota(jnp.int32, (1, pw_dev), 1)
    target = jnp.where(k == kn - 1, shift[...] - me * pw_dev, every)

    def permute_own(low, high):
        block = 256 if pw_dev % 256 == 0 else pw_dev

        def step(b, carry):
            at = pl.ds(pl.multiple_of(b * block, block), block)
            slot = lax.broadcasted_iota(jnp.int32, (block, pw_dev), 0) + b * block
            hot = jnp.where(slot == target, 1.0, 0.0).astype(jnp.bfloat16)
            for part in range(2):
                own[part, at, :] = jnp.dot(hot, wave[part], preferred_element_type=jnp.float32).astype(jnp.bfloat16)
            return carry

        lax.fori_loop(low * (pw_dev // block) // 2, high * (pw_dev // block) // 2, step, 0)

    def finish(stream):
        mine[stream] = acc[stream, me]
        ka_copy(mine.at[stream], nextb.at[stream], 1 + stream).start()

    multiply(0, 0, tiles)
    gather(0, 1 - (me & 1))
    push(0, 0)
    gather(0, me & 1)
    multiply(1, 0, 1)
    pull(0, 0)
    push(0, 1)
    multiply(1, 1, tiles)
    pull(0, 1)
    push(0, 2)
    gather(1, 1 - (me & 1))
    push(1, 0)
    pull(0, 2)
    if bits > 3:
        push(0, 3)
    gather(1, me & 1)
    pull(1, 0)
    push(1, 1)
    for stage in range(3, bits):
        pull(0, stage)
        if stage + 1 < bits:
            push(0, stage + 1)
    finish(0)
    permute_own(0, 2)
    for stage in range(1, bits - 1):
        pull(1, stage)
        push(1, stage + 1)
    wave_copy.wait()
    def plane():
        a, b = received[0], received[1]
        c, d = own[0], own[1]
        kept[0] = contract(c, a) + contract(d, b)
        kept[1] = contract(c, b) - contract(d, a)
    plane()
    pull(1, bits - 1)
    finish(1)
    for stream in range(2):
        ka_copy(mine.at[stream], nextb.at[stream], 1 + stream).wait()
    high = lax.Precision.HIGHEST
    nr = jnp.concatenate([nextb[0, :, :half], nextb[1, :, :half]], axis=1)
    ni = jnp.concatenate([nextb[0, :, half:], nextb[1, :, half:]], axis=1)
    br = jnp.concatenate([mine[0, :, :half], mine[1, :, :half]], axis=1)
    bi = jnp.concatenate([mine[0, :, half:], mine[1, :, half:]], axis=1)
    cos, sin = cosine[...], sine[...]
    charge = sym[...]
    wr = jnp.dot(charge, nr * cos + ni * sin, precision=high, preferred_element_type=jnp.float32)
    wi = jnp.dot(charge, ni * cos - nr * sin, precision=high, preferred_element_type=jnp.float32)
    kept[0] += contract(br, wr, high) + contract(bi, wi, high)
    kept[1] += contract(br, wi, high) - contract(bi, wr, high)
    share = nb // n

    def fill(count, carry):
        at = pl.ds(pl.multiple_of(count * share, share), share)
        acc_last[0, count] = kept[0, at, :]
        acc_last[1, count] = kept[1, at, :]
        return carry

    lax.fori_loop(0, n, fill, 0)
    push, pull, bits = halving(n, me, orders_of(n), *last)
    for stream in range(2):
        push(stream, 0)
    for stage in range(bits):
        for stream in range(2):
            pull(stream, stage)
            if stage + 1 < bits:
                push(stream, stage + 1)
    out[0] = acc_last[0, me]
    out[1] = acc_last[1, me]


def scatter_scratch(n, rows, cols):
    bits = n.bit_length() - 1
    return [
        pltpu.VMEM((2, n, rows, cols), jnp.float32),
        pltpu.VMEM((2, n, rows, cols), jnp.int16),
        pltpu.VMEM((2, n, rows, cols), jnp.int16),
        pltpu.VMEM((2, n, 1, cols), jnp.float32),
        pltpu.VMEM((2, n, 1, cols), jnp.float32),
        pltpu.SemaphoreType.DMA((2, 2, bits, 2)),
    ]


def vmem():
    return pl.BlockSpec(memory_space=pltpu.VMEM)


def fused(n, kn, inverse, target, cosine, sine, sym, waves, projectors):
    pw_dev, nb = waves.shape[2], waves.shape[3]
    nproj = projectors.shape[3]
    rows, share = nproj // n, nb // n
    tile = 256 if nproj % 256 == 0 else 128 if nproj % 128 == 0 else nproj
    hbm = pl.BlockSpec(memory_space=pl.ANY)
    return pl.pallas_call(
        functools.partial(fused_kernel, n, kn),
        out_shape=jax.ShapeDtypeStruct((2, share, nb), jnp.float32),
        in_specs=[pl.BlockSpec(memory_space=pltpu.SMEM), vmem(), vmem(), vmem(), vmem(), hbm, hbm],
        out_specs=vmem(),
        scratch_shapes=[
            pltpu.VMEM((2, pw_dev, nb), jnp.bfloat16),
            pltpu.VMEM((2, pw_dev, nproj), jnp.bfloat16),
            pltpu.VMEM((2, 2, pw_dev, nb), jnp.bfloat16),
            pltpu.VMEM((2, nproj, nb), jnp.float32),
            pltpu.VMEM((2, pw_dev, nb), jnp.bfloat16),
            pltpu.VMEM((2, pw_dev, nb), jnp.bfloat16),
            pltpu.VMEM((2, rows, nb), jnp.float32),
            pltpu.VMEM((2, rows, nb), jnp.float32),
            pltpu.VMEM((2, nb, nb), jnp.float32),
            pltpu.SemaphoreType.DMA((nproj // tile + 1,)),
            pltpu.SemaphoreType.DMA((2, 3)),
        ]
        + scatter_scratch(n, rows, nb)
        + scatter_scratch(n, share, nb),
        compiler_params=pltpu.CompilerParams(
            collective_id=0, has_side_effects=True, vmem_limit_bytes=62 * 2**20
        ),
    )(inverse, target, cosine, sine, sym, waves, projectors)


def invert(order, size):
    place = lax.broadcasted_iota(jnp.int32, (size, size), 0)
    slot = lax.broadcasted_iota(jnp.int32, (size, size), 1)
    return jnp.sum(jnp.where(order[:, None] == slot, place, 0), axis=0)


def local(waves, projectors, projector_order, shift_map, charges, atom_phase):
    n = lax.axis_size("pw")
    kn = lax.axis_size("ka")
    last_k = lax.axis_index("ka") == kn - 1
    pw_index = lax.axis_index("pw")
    inverse = invert(projector_order, projector_order.shape[0])
    atom_dev = atom_phase.shape[0] // n
    phase = lax.dynamic_slice_in_dim(atom_phase, pw_index * atom_dev, atom_dev)
    phase = jnp.where(last_k, phase, 0.0)
    repeated = jnp.repeat(phase, PPA)
    cosine = jnp.cos(repeated)[:, None]
    sine = jnp.sin(repeated)[:, None]
    raw = lax.dynamic_slice_in_dim(charges, pw_index * atom_dev, atom_dev, 0)
    sym = 0.5 * (raw + jnp.transpose(raw, (0, 2, 1)))
    eye = jnp.eye(atom_dev, dtype=jnp.float32)
    full = (sym[:, :, None, :] * eye[:, None, :, None]).reshape(atom_dev * PPA, atom_dev * PPA)
    summed = fused(n, kn, inverse, shift_map[None, :], cosine, sine, full, waves, projectors)
    return jnp.transpose(summed, (1, 0, 2))[None]


def solution(mesh):
    placed = (P("ka", None, "pw", None), P("ka", None, "pw", None), P(), P("pw"), P(), P())
    return jax.shard_map(
        local, mesh=mesh, in_specs=placed, out_specs=P("ka", "pw", None, None), check_vma=False
    )
```

profile of v0, /device:TPU:0, one launch (start us, length us, event | category | flops | bytes accessed | tf_op | source)
XLA Modules:
  0.0 81.5 jit_solution(8182208705233746121)
XLA Ops:
  0.0 0.0 copy-start
  0.0 0.8 fusion.2
  0.8 0.1 broadcast_in_dim.27
  0.9 0.7 cos.16.cosine
  1.6 0.1 broadcast_in_dim.28
  1.7 0.7 sin.16.sine
  2.4 0.0 copy-done
  2.4 0.1 constant_dynamic-slice_fusion
  2.5 0.1 fusion
  2.6 0.2 copy.16
  2.8 0.1 broadcast_multiply_fusion
  2.9 0.9 %mul.33.sym = f32[144,144]{1,0:T(8,128)} reshape(f32[8,18,8,18]{3,2,1,0:T(8,128)S(1)} %broadcast_multiply_fusion) | data formatting | bytes 165888 | tf_op jit(solution)/shard_map/mul | solution.py:345
  3.7 3.5 %select_reduce_fusion.inverse = s32[2304]{0:T(1024)} fusion(s32[2304]{0:T(1024)} %param.8), kind=kLoop, calls=%fused_computation | loop fusion | flops 15922944 | bytes 18432 | tf_op jit(solution)/shard_map/reduce_sum | solution.py:327
  7.2 72.9 %shard_map.64 = f32[2,16,256]{2,1,0:T(8,128)} custom-call(s32[2304]{0:T(1024)} %select_reduce_fusion.inverse, s32[1,2048]{1,0:T(1,128)} %bitcast.11, f32[144,1]{1,0:T(8,128)} %cos.16.cosine, f32[144,1]{1,0:T(8,128)} %sin.16.sine, f32[144,144]{1,0:T(8,128)} %mul.33.sym, bf16[1,2,2048,256]{3,2,1,0:T(8,128)(2,1)} %wave_hbm.1, bf16[1,2,2048,2304]{3,2,1,0:T(8,128)(2,1)} %beta_hbm.1), custom_call_target="tpu_custom_call" | custom-call | tf_op jit(solution)/shard_map/pallas_call | solution.py:298
  80.1 1.4 %copy.19 = f32[1,16,2,256]{3,2,1,0:T(2,128)} copy(f32[1,16,2,256]{3,1,2,0:T(8,128)} %bitcast.10) | data formatting | bytes 65536 | tf_op jit(solution)/shard_map/broadcast_in_dim | solution.py:347
  (1 shorter events, 0.0 us)
Async XLA Ops:
  0.0 2.4 %copy-start = (f32[128,18,18]{0,2,1:T(8,128)S(1)}, f32[128,18,18]{0,2,1:T(8,128)}, u32[]{:S(2)}) copy-start(f32[128,18,18]{0,2,1:T(8,128)} %param.10) | copy-start | bytes 497668
where the time goes:
time: 81.8 us; the launch traced here: 81.5 us
  Pallas kernels  72.9 us (89%)
  other arithmetic  4.45 us (5%)
  local copies, waits for them, and re-layouts  4.14 us (5%)
    pallas_call x1, Pallas kernels, fused(): pl.pallas_call(functools.partial(fused_kernel, n, kn), out_shape=jax.Shap...  72.9 us
    reduce_sum x1, other arithmetic, invert(): return jnp.sum(jnp.where(order[:, None] == slot, place, 0), axis=0)  3.48 us

commit v1 on v0

v1 whole, which is shorter than its diff:
```python
import functools

import jax
import jax.numpy as jnp
from jax import lax
from jax.experimental import pallas as pl
from jax.experimental.pallas import tpu as pltpu
from jax.sharding import PartitionSpec as P

MESH = pl.DeviceIdType.MESH
LANES = 128
TOP = 32767.0
HIGH = lax.Precision.HIGHEST


def dot(left, right, dims, precision=None):
    return lax.dot_general(
        left, right, (((dims[0],), (dims[1],)), ((), ())),
        precision=precision, preferred_element_type=jnp.float32,
    )


def contract(left, right, precision=None):
    return dot(left, right, (0, 0), precision)


def cross(left, right):
    real = contract(left[0], right[0]) + contract(left[1], right[1])
    imag = contract(left[0], right[1]) - contract(left[1], right[0])
    return real, imag


def low(v):
    return jnp.right_shift(jnp.left_shift(v, 16), 16).astype(jnp.float32)


def high(v):
    return jnp.right_shift(v, 16).astype(jnp.float32)


def code(x, inv):
    return jnp.floor(x * inv + 0.5).astype(jnp.int32)


def pack(real, imag, inv_real, inv_imag):
    return jnp.bitwise_or(
        jnp.left_shift(code(imag, inv_imag), 16),
        jnp.bitwise_and(code(real, inv_real), 0xFFFF),
    )


def fold(x):
    return jnp.max(jnp.abs(x).reshape(x.shape[0] // 8, 8, x.shape[1]), axis=0)


def scale_of(top):
    return jnp.maximum(jnp.max(top, axis=0, keepdims=True), 1e-30) * (1.0 / TOP)


def block_of(size):
    for block in (512, 256, 128):
        if size % block == 0:
            return block
    return size


def fused_kernel(
    n, kn, ppa, order_hbm, shift_hbm, phase_hbm, charge_hbm, wave_hbm, beta_hbm, out,
    order, shift, phase, charge, inv_v, inv_s, spread, sym, wave, beta, rhs, proj_t, top, inv_b, packed,
    gs, go, cr, sc0, sc0_r, xf, xs, xr, scx, scx_r, acc, zs, zr, scz, scz_r, mine, ys, yr, scy, scy_r,
    wr, picked, stage, part, ms, mr, scm, scm_r, macc, ds, dr, scd, scd_r,
    local_sems, core_sems, core_scale_sems, x_sems, z_sems, y_sems, wave_sems, m_sems, d_sems,
):
    me = lax.axis_index("pw")
    k = lax.axis_index("ka")
    ahead, behind = lax.rem(k + 1, kn), lax.rem(k + kn - 1, kn)
    last_k = k == kn - 1
    paired = kn == 2
    pw_dev, nb = wave.shape[1], wave.shape[2]
    nproj = beta.shape[2]
    streams = nb // LANES
    rows = gs.shape[2]
    parts = 2 if rows % 16 == 0 else 1
    rs = rows // parts
    halfn, zn = n // 2, n // 4
    share = nb // n
    core, xbit, mez, mej = me & 1, (me >> 1) & 1, me >> 2, me >> 1
    tile = block_of(nproj) if nproj % 256 else 256
    tiles = nproj // tile
    third = wr.shape[2]

    def beta_copy(t):
        at = pl.ds(pl.multiple_of(t * tile, tile), tile)
        return pltpu.make_async_copy(beta_hbm.at[0, :, :, at], beta.at[:, :, at], local_sems.at[t])

    small = [
        pltpu.make_async_copy(src, dst, local_sems.at[tiles + i])
        for i, (src, dst) in enumerate((
            (order_hbm, order), (wave_hbm.at[0], wave), (shift_hbm, shift), (phase_hbm, phase),
            (charge_hbm, charge.at[:, pl.ds(0, ppa), :]), (inv_v, inv_s),
        ))
    ]
    for copy in small[:2]:
        copy.start()
    for t in range(tiles):
        beta_copy(t).start()
    for copy in small[2:5]:
        copy.start()

    barrier = pltpu.get_barrier_semaphore()
    greet = [{"pw": me ^ 1}] + [{"pw": me ^ (d << 1)} for d in range(1, halfn)]
    if paired:
        greet += [{"ka": ahead, "pw": me ^ (d << 1)} for d in range(halfn)]
    else:
        greet += [{"ka": ahead}, {"ka": behind}]
    for where in greet:
        pl.semaphore_signal(barrier, inc=1, device_id=where, device_id_type=MESH)

    def remote(src, dst, send, recv, where):
        return pltpu.make_async_remote_copy(
            src_ref=src, dst_ref=dst, send_sem=send, recv_sem=recv,
            device_id=where, device_id_type=MESH,
        )

    def invert():
        blocks = inv_v.shape[0]
        small[0].wait()
        slots = order[...]
        upper, lower = jnp.right_shift(slots, 7), jnp.bitwise_and(slots, 127)
        place = lax.broadcasted_iota(jnp.int32, (1, nproj), 1)
        hot_u = lax.broadcasted_iota(jnp.int32, (blocks, nproj), 0) == upper
        hot_l = lax.broadcasted_iota(jnp.int32, (LANES, nproj), 0) == lower
        coarse = jnp.right_shift(place, 4).astype(jnp.float32)
        fine = jnp.bitwise_and(place, 15).astype(jnp.float32)
        left = jnp.concatenate([jnp.where(hot_u, coarse, 0.0), jnp.where(hot_u, fine, 0.0)], axis=0)
        found = dot(left.astype(jnp.bfloat16), jnp.where(hot_l, 1.0, 0.0).astype(jnp.bfloat16), (1, 1))
        found = (found[:blocks] * 16.0 + found[blocks:] + 0.5).astype(jnp.int32)
        inv_v[...] = jnp.clip(found, 0, nproj - 1)
        small[5].start()

    def transpose_waves():
        small[1].wait()
        for p in range(2):
            flat = wave[p].T
            for h in range(streams):
                mid = flat[h * LANES : (h + 1) * LANES]
                rhs[h, p, :LANES, :] = mid
                rhs[h, 1 - p, LANES:, :] = mid if p else -mid

    def multiply(h):
        top[...] = jnp.zeros_like(top)

        def step(t, carry):
            if h == 0:
                beta_copy(t).wait()
            at = pl.ds(pl.multiple_of(t * tile, tile), tile)
            got = dot(rhs[h, 0], beta[0, :, at], (1, 0)) + dot(rhs[h, 1], beta[1, :, at], (1, 0))
            proj_t[:, at] = got
            peak = top[...]
            for b in range(tile // LANES):
                peak = jnp.maximum(peak, jnp.abs(got[:, b * LANES : (b + 1) * LANES]))
            top[...] = peak
            return carry

        lax.fori_loop(0, tiles, step, 0)

    def encode(h):
        peak = jnp.max(top[...], axis=1, keepdims=True)
        scale = jnp.maximum(peak, 1e-30) * (1.0 / TOP)
        inv_b[...] = jnp.broadcast_to(1.0 / scale, inv_b.shape)
        flat = jnp.broadcast_to(scale, inv_b.shape)
        sc0[h, 0:1, :] = flat[:LANES].T[0:1]
        sc0[h, 1:2, :] = flat[LANES:].T[0:1]

        def step(t, carry):
            at = pl.ds(pl.multiple_of(t * LANES, LANES), LANES)
            coded = pack(proj_t[:LANES, at], proj_t[LANES:, at], inv_b[:LANES], inv_b[LANES:])
            packed[at, :] = coded.T
            return carry

        lax.fori_loop(0, nproj // LANES, step, 0)

    def gather(dst, h, parity, sub):
        def one(j, carry):
            base = ((j << 1) | parity) * rows + sub * rs
            for g in range(rs // 8):
                slot = base + 8 * g
                upper, lower = slot >> 7, slot & 127
                taken = [packed[pl.ds(inv_s[upper, lower + r], 1), :] for r in range(8)]
                dst[h, j, pl.ds(sub * rs + 8 * g, 8), :] = jnp.concatenate(taken, axis=0)
            return carry

        lax.fori_loop(0, halfn, one, 0)

    def span(sub):
        return pl.ds(sub * rs, rs)

    def core_copy(h, sub):
        return remote(
            gs.at[h, :, span(sub)], cr.at[h, :, span(sub)],
            core_sems.at[0, h, sub], core_sems.at[1, h, sub], {"pw": me ^ 1},
        )

    def core_scale_copy(h):
        return remote(sc0.at[h], sc0_r.at[h], core_scale_sems.at[0, h], core_scale_sems.at[1, h], {"pw": me ^ 1})

    def x_copies(h, sub):
        sems, where = x_sems, {"pw": me ^ 2}
        return [
            remote(xs.at[h, :, span(sub)], xr.at[h, :, span(sub)], sems.at[0, h, sub, 0], sems.at[1, h, sub, 0], where),
            remote(scx.at[h, sub], scx_r.at[h, sub], sems.at[0, h, sub, 1], sems.at[1, h, sub, 1], where),
        ]

    def z_copies(h, sub):
        made = []
        for d in range(1, zn):
            where = {"pw": me ^ (d << 2)}
            made.append(remote(
                zs.at[h, d - 1, span(sub)], zr.at[h, d - 1, span(sub)],
                z_sems.at[0, h, sub, d - 1, 0], z_sems.at[1, h, sub, d - 1, 0], where,
            ))
            made.append(remote(
                scz.at[h, sub], scz_r.at[h, sub, d - 1],
                z_sems.at[0, h, sub, d - 1, 1], z_sems.at[1, h, sub, d - 1, 1], where,
            ))
        return made

    def y_copies(h, sub):
        where = {"ka": behind}
        return [
            remote(ys.at[h, span(sub)], yr.at[h, span(sub)], y_sems.at[0, h, sub, 0], y_sems.at[1, h, sub, 0], where),
            remote(scy.at[h, sub], scy_r.at[h, sub], y_sems.at[0, h, sub, 1], y_sems.at[1, h, sub, 1], where),
        ]

    none = jnp.zeros((8, LANES), jnp.float32)

    def put_scale(ref, h, sub, tops):
        scales = [scale_of(t) for t in tops]
        ref[h, sub, 0:1, :] = scales[0]
        ref[h, sub, 1:2, :] = scales[1]
        return [1.0 / s for s in scales]

    def send_core(h, sub):
        gather(gs, h, 1 - core, sub)
        if sub == 0:
            core_scale_copy(h).start()
        core_copy(h, sub).start()

    def step_core(h, sub):
        if sub == 0:
            core_scale_copy(h).wait()
        core_copy(h, sub).wait()
        at = span(sub)
        own_r, own_i = sc0[h, 0:1, :], sc0[h, 1:2, :]
        sib_r, sib_i = sc0_r[h, 0:1, :], sc0_r[h, 1:2, :]

        def total(j):
            a, b = go[h, j, at, :], cr[h, j, at, :]
            return low(a) * own_r + low(b) * sib_r, high(a) * own_i + high(b) * sib_i

        def first(z, carry):
            tr, ti = carry
            real, imag = total((z << 1) | (1 - xbit))
            xf[z, 0], xf[z, 1] = real, imag
            return jnp.maximum(tr, fold(real)), jnp.maximum(ti, fold(imag))

        inv = put_scale(scx, h, sub, lax.fori_loop(0, zn, first, (none, none)))

        def second(z, carry):
            xs[h, z, at, :] = pack(xf[z, 0], xf[z, 1], *inv)
            return carry

        lax.fori_loop(0, zn, second, 0)
        for copy in x_copies(h, sub):
            copy.start()

        def keep(z, carry):
            real, imag = total((z << 1) | xbit)
            acc[h, z, 0, at, :] = real
            acc[h, z, 1, at, :] = imag
            return carry

        lax.fori_loop(0, zn, keep, 0)

    def step_x(h, sub):
        for copy in x_copies(h, sub):
            copy.wait()
        at = span(sub)
        s_r, s_i = scx_r[h, sub, 0:1, :], scx_r[h, sub, 1:2, :]

        def total(z):
            v = xr[h, z, at, :]
            real = acc[h, z, 0, at, :] + low(v) * s_r
            imag = acc[h, z, 1, at, :] + high(v) * s_i
            acc[h, z, 0, at, :] = real
            acc[h, z, 1, at, :] = imag
            return real, imag

        def first(d, carry):
            tr, ti = carry
            real, imag = total(mez ^ d)
            return jnp.maximum(tr, fold(real)), jnp.maximum(ti, fold(imag))

        inv = put_scale(scz, h, sub, lax.fori_loop(1, zn, first, (none, none)))

        def second(d, carry):
            z = mez ^ d
            zs[h, d - 1, at, :] = pack(acc[h, z, 0, at, :], acc[h, z, 1, at, :], *inv)
            return carry

        lax.fori_loop(1, zn, second, 0)
        for copy in z_copies(h, sub):
            copy.start()
        total(mez)

    def step_z(h, sub):
        for copy in z_copies(h, sub):
            copy.wait()
        at = span(sub)
        real, imag = acc[h, mez, 0, at, :], acc[h, mez, 1, at, :]
        for d in range(zn - 1):
            v = zr[h, d, at, :]
            real = real + low(v) * scz_r[h, sub, d, 0:1, :]
            imag = imag + high(v) * scz_r[h, sub, d, 1:2, :]
        cols = slice(h * LANES, (h + 1) * LANES)
        mine[0, at, cols] = real
        mine[1, at, cols] = imag
        inv = put_scale(scy, h, sub, (fold(real), fold(imag)))
        ys[h, at, :] = pack(real, imag, *inv)
        for copy in y_copies(h, sub):
            copy.start()

    def wave_copy(i, src):
        return remote(src, wr.at[i], wave_sems.at[0, i], wave_sems.at[1, i], {"ka": behind})

    def own_rows(i):
        return wave_hbm.at[0, :, pl.ds(i * third, third), :]

    def send_waves():
        if not paired:
            wave_copy(0, wave_hbm.at[0]).start()
            return

        @pl.when(k == 0)
        def _():
            wave_copy(0, own_rows(3)).start()

        @pl.when(k == 1)
        def _():
            for i in range(3):
                wave_copy(i, own_rows(i)).start()

    def spread_shift():
        small[2].wait()
        for b in range(pw_dev // LANES):
            line = shift[0:1, b * LANES : (b + 1) * LANES] - me * pw_dev
            spread[pl.ds(b * LANES, LANES), :] = jnp.broadcast_to(line, (LANES, LANES)).T

    def permute(dst, src, start, size, offset):
        block = min(block_of(size), 256)

        def step(b, carry):
            at = pl.ds(pl.multiple_of(start + b * block, block), block)
            to = pl.ds(pl.multiple_of(offset + b * block, block), block)
            want = spread[at, :]
            lane = lax.broadcasted_iota(jnp.int32, (block, LANES), 1)
            hot = jnp.concatenate(
                [jnp.where(want == lane + g * LANES, 1.0, 0.0) for g in range(pw_dev // LANES)], axis=1
            ).astype(jnp.bfloat16)
            for p in range(2):
                dst[p, to, :] = dot(hot, src(p), (1, 0)).astype(jnp.bfloat16)
            return carry

        lax.fori_loop(0, size // block, step, 0)

    def send_picked():
        @pl.when(k == 0)
        def _():
            permute(stage, lambda p: wave[p], 3 * third, third, 0)
            wave_copy(1, stage).start()

    def build_picked():
        @pl.when(k == 0)
        def _():
            permute(picked, lambda p: wave[p], 0, 3 * third, 0)

    def add(which, values, fresh):
        for c in range(2):
            if fresh:
                part[which, c] = values[c]
            else:
                part[which, c] += values[c]

    def piece(ref, i):
        return [ref[p, i * third : (i + 1) * third, :] for p in range(2)]

    def plane_first(i):
        @pl.when(k == 0)
        def _():
            wave_copy(i, own_rows(i)).wait_recv()
            got = [wr[i, 0], wr[i, 1]]
            add(0, cross(piece(wave, i), got), i == 0)
            add(1, cross(got, piece(picked, i)), i == 0)

    def plane_second(i):
        @pl.when(k == 1)
        def _():
            wave_copy(i, own_rows(i)).wait_recv()
            got = [wr[i, 0], wr[i, 1]]
            if i == 0:
                add(1, cross(got, piece(wave, 3)), True)
            else:
                add(0, cross(piece(wave, 3), got), True)

    def drain_waves():
        if not paired:
            wave_copy(0, wave_hbm.at[0]).wait_send()
            return

        @pl.when(k == 0)
        def _():
            wave_copy(0, own_rows(3)).wait_send()
            wave_copy(1, stage).wait_send()

        @pl.when(k == 1)
        def _():
            for i in range(3):
                wave_copy(i, own_rows(i)).wait_send()

    def plane_ring():
        wave_copy(0, wave_hbm.at[0]).wait_recv()

        @pl.when(last_k)
        def _():
            permute(picked, lambda p: wr[0, p], 0, pw_dev, 0)

        @pl.when(k != kn - 1)
        def _():
            picked[...] = wr[0]

        add(0, cross([wave[0], wave[1]], [picked[0], picked[1]]), True)

    def make_tables():
        small[3].wait()
        small[4].wait()
        atoms = phase.shape[1]
        own_atoms = rows // ppa
        row_i = lax.broadcasted_iota(jnp.int32, (rows, atoms), 0)
        lane = lax.broadcasted_iota(jnp.int32, (rows, atoms), 1)
        away = row_i - ppa * (lane - me * own_atoms)
        hit = (away >= 0) & (away < ppa)
        angle = jnp.where(last_k, phase[...], 0.0)
        cosine = jnp.sum(jnp.where(hit, jnp.cos(angle), 0.0), axis=1, keepdims=True)
        sine = jnp.sum(jnp.where(hit, jnp.sin(angle), 0.0), axis=1, keepdims=True)
        pad = charge.shape[1]
        flat = charge[...].reshape(ppa * pad, atoms)
        pick = jnp.where(hit, 1.0, 0.0)
        every = dot(pick, flat, (1, 1), HIGH)

        def iota(shape, axis):
            return lax.broadcasted_iota(jnp.int32, shape, axis).astype(jnp.float32)

        def div(x, by):
            return jnp.floor((x + 0.5) * (1.0 / by))

        shape = (rows, ppa * pad)
        r, c = iota(shape, 0), iota(shape, 1)
        own_p = r - ppa * div(r, ppa)
        col_p = div(c, pad)
        kept = jnp.where((own_p == col_p) & (c - pad * col_p < ppa), every, 0.0)
        shape = (ppa * pad, rows)
        c, j = iota(shape, 0), iota(shape, 1)
        widen = jnp.where(c - pad * div(c, pad) == j - ppa * div(j, ppa), 1.0, 0.0)
        full = dot(kept, widen, (1, 0), HIGH) + dot(widen, kept, (0, 1), HIGH)
        shape = (rows, rows)
        same = div(iota(shape, 0), ppa) == div(iota(shape, 1), ppa)
        sym[...] = jnp.where(same, 0.5 * full, 0.0)
        return cosine, sine

    def m_copies(w):
        where = {"pw": me ^ 1}
        return [
            remote(ms.at[w], mr.at[w], m_sems.at[0, w, 0], m_sems.at[1, w, 0], where),
            remote(scm.at[w], scm_r.at[w], m_sems.at[0, w, 1], m_sems.at[1, w, 1], where),
        ]

    def d_copies(w):
        made = []
        for d in range(1 - w, halfn):
            where = {"pw": me ^ (d << 1)}
            if w:
                where["ka"] = ahead
            made.append(remote(
                ds.at[w, d], dr.at[w, d], d_sems.at[0, w, d, 0], d_sems.at[1, w, d, 0], where,
            ))
            made.append(remote(
                scd.at[w], scd_r.at[w, d], d_sems.at[0, w, d, 1], d_sems.at[1, w, d, 1], where,
            ))
        return made

    wide = jnp.zeros((8, nb), jnp.float32)

    def block_at(j, parity):
        return pl.ds(pl.multiple_of(((j << 1) | parity) * share, share), share)

    def margin_scale(ref, w, tops):
        scales = [scale_of(t) for t in tops]
        ref[w, 0:1, :] = scales[0]
        ref[w, 1:2, :] = scales[1]
        return [1.0 / s for s in scales]

    def send_margin(w):
        def first(j, carry):
            at = block_at(j, 1 - core)
            return jnp.maximum(carry[0], fold(part[w, 0, at, :])), jnp.maximum(carry[1], fold(part[w, 1, at, :]))

        inv = margin_scale(scm, w, lax.fori_loop(0, halfn, first, (wide, wide)))

        def second(j, carry):
            at = block_at(j, 1 - core)
            ms[w, j] = pack(part[w, 0, at, :], part[w, 1, at, :], *inv)
            return carry

        lax.fori_loop(0, halfn, second, 0)
        for copy in m_copies(w):
            copy.start()

    def step_margin(w):
        for copy in m_copies(w):
            copy.wait()
        s_r, s_i = scm_r[w, 0:1, :], scm_r[w, 1:2, :]

        def first(d, carry):
            j = mej ^ d
            at = block_at(j, core)
            v = mr[w, j]
            real = part[w, 0, at, :] + low(v) * s_r
            imag = part[w, 1, at, :] + high(v) * s_i
            macc[w, d, 0], macc[w, d, 1] = real, imag
            return jnp.maximum(carry[0], fold(real)), jnp.maximum(carry[1], fold(imag))

        inv = margin_scale(scd, w, lax.fori_loop(0, halfn, first, (wide, wide)))

        def second(d, carry):
            ds[w, d] = pack(macc[w, d, 0], macc[w, d, 1], *inv)
            return carry

        lax.fori_loop(1 - w, halfn, second, 0)
        for copy in d_copies(w):
            copy.start()

    def finish_margin(w, real, imag):
        for copy in d_copies(w):
            copy.wait()
        for d in range(1 - w, halfn):
            v = dr[w, d]
            real = real + low(v) * scd_r[w, d, 0:1, :]
            imag = imag + high(v) * scd_r[w, d, 1:2, :]
        return real, imag

    last = streams - 1
    invert()
    transpose_waves()
    pl.semaphore_wait(barrier, len(greet))
    send_waves()
    small[5].wait()
    for h in range(streams):
        multiply(h)
        encode(h)
        for sub in range(parts):
            send_core(h, sub)
        for sub in range(parts):
            gather(go, h, core, sub)
            step_core(h, sub)
            if h > 0:
                step_x(h - 1, sub)
    spread_shift()
    if paired:
        send_picked()
        build_picked()
        plane_first(0)
        plane_second(0)
        plane_first(1)
    cosine, sine = make_tables()
    step_x(last, 0)
    for h in range(last):
        for sub in range(parts):
            step_z(h, sub)
    for sub in range(1, parts):
        step_x(last, sub)
    if paired:
        plane_first(2)
        send_margin(1)
    for sub in range(parts):
        step_z(last, sub)
    if paired:
        step_margin(1)
        plane_second(1)
    else:
        plane_ring()
    for h in range(streams):
        for sub in range(parts):
            for copy in y_copies(h, sub):
                copy.wait()

    def next_part(take, c):
        lines = []
        for sub in range(parts):
            pieces = [take(yr[h, span(sub), :]) * scy_r[h, sub, c : c + 1, :] for h in range(streams)]
            lines.append(jnp.concatenate(pieces, axis=1))
        return jnp.concatenate(lines, axis=0)

    nr, ni = next_part(low, 0), next_part(high, 1)
    turned = jnp.concatenate([nr * cosine + ni * sine, ni * cosine - nr * sine], axis=1)
    weighted = dot(sym[...], turned, (1, 0), HIGH)
    by_real = contract(mine[0], weighted, HIGH)
    by_imag = contract(mine[1], weighted, HIGH)
    part[0, 0] += by_real[:, :nb] + by_imag[:, nb:]
    part[0, 1] += by_real[:, nb:] - by_imag[:, :nb]
    send_margin(0)
    step_margin(0)
    real, imag = macc[0, 0, 0], macc[0, 0, 1]
    if paired:
        real, imag = finish_margin(1, real, imag)
    real, imag = finish_margin(0, real, imag)
    drain_waves()
    out[0] = real
    out[1] = imag


def fused(n, kn, order, shift, phase, charges, waves, projectors):
    pw_dev, nb = waves.shape[2], waves.shape[3]
    nproj = projectors.shape[3]
    atoms = phase.shape[1]
    ppa = charges.shape[0]
    rows, share = nproj // n, nb // n
    h = nb // LANES
    parts = 2 if rows % 16 == 0 else 1
    zn, half = n // 4, n // 2
    pad = -(-ppa // 8) * 8
    blocks = -(-nproj // (8 * LANES)) * 8
    paired = kn == 2
    slots, third = (3, pw_dev // 4) if paired else (1, pw_dev)
    kinds = 2 if paired else 1
    anywhere = pl.BlockSpec(memory_space=pl.ANY)
    f32, i32, bf16 = jnp.float32, jnp.int32, jnp.bfloat16
    tile = block_of(nproj) if nproj % 256 else 256
    scratch = [
        ((1, nproj), i32), ((1, pw_dev), i32), ((1, atoms), f32), ((ppa, pad, atoms), f32),
        ((blocks, LANES), i32), "smem", ((pw_dev, LANES), i32), ((rows, rows), f32),
        ((2, pw_dev, nb), bf16), ((2, pw_dev, nproj), bf16), ((h, 2, 2 * LANES, pw_dev), bf16),
        ((2 * LANES, nproj), f32), ((2 * LANES, LANES), f32), ((2 * LANES, LANES), f32), ((nproj, LANES), i32),
        ((h, half, rows, LANES), i32), ((h, half, rows, LANES), i32), ((h, half, rows, LANES), i32),
        ((h, 2, LANES), f32), ((h, 2, LANES), f32),
        ((zn, 2, rows // parts, LANES), f32), ((h, zn, rows, LANES), i32), ((h, zn, rows, LANES), i32),
        ((h, parts, 2, LANES), f32), ((h, parts, 2, LANES), f32), ((h, zn, 2, rows, LANES), f32),
        ((h, zn - 1, rows, LANES), i32), ((h, zn - 1, rows, LANES), i32),
        ((h, parts, 2, LANES), f32), ((h, parts, zn - 1, 2, LANES), f32), ((2, rows, nb), f32),
        ((h, rows, LANES), i32), ((h, rows, LANES), i32), ((h, parts, 2, LANES), f32), ((h, parts, 2, LANES), f32),
        ((slots, 2, third, nb), bf16), ((2, slots * third, nb), bf16), ((2, third, nb), bf16),
        ((kinds, 2, nb, nb), f32), ((kinds, half, share, nb), i32), ((kinds, half, share, nb), i32),
        ((kinds, 2, nb), f32), ((kinds, 2, nb), f32), ((kinds, half, 2, share, nb), f32),
        ((kinds, half, share, nb), i32), ((kinds, half, share, nb), i32),
        ((kinds, 2, nb), f32), ((kinds, half, 2, nb), f32),
    ]
    made = [pltpu.SMEM((blocks, LANES), i32) if s == "smem" else pltpu.VMEM(*s) for s in scratch]
    sems = [
        (nproj // tile + 6,), (2, h, parts), (2, h), (2, h, parts, 2), (2, h, parts, zn - 1, 2),
        (2, h, parts, 2), (2, slots), (2, kinds, 2), (2, kinds, half, 2),
    ]
    return pl.pallas_call(
        functools.partial(fused_kernel, n, kn, ppa),
        out_shape=jax.ShapeDtypeStruct((2, share, nb), f32),
        in_specs=[anywhere] * 6,
        out_specs=pl.BlockSpec(memory_space=pltpu.VMEM),
        scratch_shapes=made + [pltpu.SemaphoreType.DMA(s) for s in sems],
        compiler_params=pltpu.CompilerParams(
            collective_id=0, has_side_effects=True, vmem_limit_bytes=62 * 2**20
        ),
    )(order, shift, phase, charges, waves, projectors)


def local(waves, projectors, projector_order, shift_map, charges, atom_phase):
    n = lax.axis_size("pw")
    kn = lax.axis_size("ka")
    summed = fused(
        n, kn, projector_order[None, :], shift_map[None, :], atom_phase[None, :],
        jnp.transpose(charges, (1, 2, 0)), waves, projectors,
    )
    return jnp.transpose(summed, (1, 0, 2))[None]


def solution(mesh):
    placed = (P("ka", None, "pw", None), P("ka", None, "pw", None), P(), P("pw"), P(), P())
    return jax.shard_map(
        local, mesh=mesh, in_specs=placed, out_specs=P("ka", "pw", None, None), check_vma=False
    )
```

time: 81.8 us -> 69.5 us (0.85)
  Pallas kernels: 72.9 us -> 66.5 us
  other arithmetic: 4.45 us -> 0 us
  local copies, waits for them, and re-layouts: 4.14 us -> 2.71 us
    pallas_call x1, Pallas kernels: 72.9 us -> 66.5 us  [fused(): pl.pallas_call(functools.partial(fused_kernel, n, kn, ppa), out_shape=jax...]
    reduce_sum x1 -> x0, other arithmetic: 3.48 us -> none  [invert(): return jnp.sum(jnp.where(order[:, None] == slot, place, 0), axis=0)]
    broadcast_in_dim x2 -> x1, local copies, waits for them, and re-layouts: 0.14 us -> 1.31 us  [local(): projector_order[None, :]]
    mul x2 -> x0, local copies, waits for them, and re-layouts: 1.04 us -> none  [the longest x1 0.85 us: local(): sym[:, :, None, :] * eye[:, None, :, None]]
where the time goes in v1:
time: 69.5 us; the launch traced here: 69.3 us
  Pallas kernels  66.5 us (96%)
  local copies, waits for them, and re-layouts  2.71 us (4%)
    pallas_call x1, Pallas kernels, fused(): pl.pallas_call(functools.partial(fused_kernel, n, kn, ppa), out_shape=jax...  66.5 us
    broadcast_in_dim x1, local copies, waits for them, and re-layouts, local(): return jnp.transpose(summed, (1, 0, 2))[None]  1.4 us

profile of v1, /device:TPU:0, one launch (start us, length us, event | category | flops | bytes accessed | tf_op | source)
XLA Modules:
  0.0 69.3 jit_solution(7043866384649935215)
XLA Ops:
  0.0 1.3 %broadcast_in_dim.12.order_hbm = s32[1,2304]{1,0:T(1,128)} reshape(s32[2304]{0:T(1024)} %param.8) | data formatting | bytes 18432 | tf_op jit(solution)/shard_map/broadcast_in_dim | solution.py:687
  1.3 66.5 %shard_map.64 = f32[2,16,256]{2,1,0:T(8,128)} custom-call(s32[1,2304]{1,0:T(1,128)} %broadcast_in_dim.12.order_hbm, s32[1,2048]{1,0:T(1,128)} %bitcast.8, f32[1,128]{1,0:T(1,128)} %bitcast.9, f32[18,18,128]{2,1,0:T(8,128)} %bitcast.6, bf16[1,2,2048,256]{3,2,1,0:T(8,128)(2,1)} %wave_hbm.1, bf16[1,2,2048,2304]{3,2,1,0:T(8,128)(2,1)} %beta_hbm.1), custom_call_target="tpu_custom_call" | custom-call | tf_op jit(solution)/shard_map/pallas_call | solution.py:671
  67.9 1.4 %copy.7 = f32[1,16,2,256]{3,2,1,0:T(2,128)} copy(f32[1,16,2,256]{3,1,2,0:T(8,128)} %bitcast.7) | data formatting | bytes 65536 | tf_op jit(solution)/shard_map/broadcast_in_dim | solution.py:690

commit v2 on v1

--- a/solution.py
+++ b/solution.py
@@ -97,25 +97,27 @@
         pltpu.make_async_copy(src, dst, local_sems.at[tiles + i])
         for i, (src, dst) in enumerate((
             (order_hbm, order), (wave_hbm.at[0], wave), (shift_hbm, shift), (phase_hbm, phase),
-            (charge_hbm, charge.at[:, pl.ds(0, ppa), :]), (inv_v, inv_s),
+            (charge_hbm, charge.at[:, pl.ds(0, ppa), :]),
         ))
     ]
+    barrier = pltpu.get_barrier_semaphore()
+    greet = [{"pw": me ^ 1}, {"pw": me ^ 2}] + [{"pw": me ^ (d << 2)} for d in range(1, zn)]
+    greet += [{"ka": ahead}] if paired else [{"ka": ahead}, {"ka": behind}]
+    for where in greet:
+        pl.semaphore_signal(barrier, inc=1, device_id=where, device_id_type=MESH)
+
     for copy in small[:2]:
         copy.start()
-    for t in range(tiles):
+    depth = min(4, tiles)
+    for t in range(depth):
         beta_copy(t).start()
     for copy in small[2:5]:
         copy.start()
 
-    barrier = pltpu.get_barrier_semaphore()
-    greet = [{"pw": me ^ 1}] + [{"pw": me ^ (d << 1)} for d in range(1, halfn)]
-    if paired:
-        greet += [{"ka": ahead, "pw": me ^ (d << 1)} for d in range(halfn)]
-    else:
-        greet += [{"ka": ahead}, {"ka": behind}]
-    for where in greet:
-        pl.semaphore_signal(barrier, inc=1, device_id=where, device_id_type=MESH)
-
+    inverse_copies = [
+        pltpu.make_async_copy(inv_v.at[b], inv_s.at[pl.ds(b * LANES, LANES)], local_sems.at[tiles + 5 + b])
+        for b in range(inv_v.shape[0])
+    ]
     def remote(src, dst, send, recv, where):
         return pltpu.make_async_remote_copy(
             src_ref=src, dst_ref=dst, send_sem=send, recv_sem=recv,
@@ -125,7 +127,7 @@
     def invert():
         blocks = inv_v.shape[0]
         small[0].wait()
-        slots = order[...]
+        slots = jnp.concatenate([order[r : r + 1, :] for r in range(nproj // LANES)], axis=1)
         upper, lower = jnp.right_shift(slots, 7), jnp.bitwise_and(slots, 127)
         place = lax.broadcasted_iota(jnp.int32, (1, nproj), 1)
         hot_u = lax.broadcasted_iota(jnp.int32, (blocks, nproj), 0) == upper
@@ -136,7 +138,8 @@
         found = dot(left.astype(jnp.bfloat16), jnp.where(hot_l, 1.0, 0.0).astype(jnp.bfloat16), (1, 1))
         found = (found[:blocks] * 16.0 + found[blocks:] + 0.5).astype(jnp.int32)
         inv_v[...] = jnp.clip(found, 0, nproj - 1)
-        small[5].start()
+        for copy in inverse_copies:
+            copy.start()
 
     def transpose_waves():
         small[1].wait()
@@ -147,25 +150,29 @@
                 rhs[h, p, :LANES, :] = mid
                 rhs[h, 1 - p, LANES:, :] = mid if p else -mid
 
-    def multiply(h):
-        top[...] = jnp.zeros_like(top)
-
+    def multiply(hs, start, stop):
         def step(t, carry):
-            if h == 0:
+            if 0 in hs:
                 beta_copy(t).wait()
+
+                @pl.when(t + depth < tiles)
+                def _():
+                    beta_copy(t + depth).start()
+
             at = pl.ds(pl.multiple_of(t * tile, tile), tile)
-            got = dot(rhs[h, 0], beta[0, :, at], (1, 0)) + dot(rhs[h, 1], beta[1, :, at], (1, 0))
-            proj_t[:, at] = got
-            peak = top[...]
-            for b in range(tile // LANES):
-                peak = jnp.maximum(peak, jnp.abs(got[:, b * LANES : (b + 1) * LANES]))
-            top[...] = peak
-            return carry
-
-        lax.fori_loop(0, tiles, step, 0)
+            for h in hs:
+                got = dot(rhs[h, 0], beta[0, :, at], (1, 0)) + dot(rhs[h, 1], beta[1, :, at], (1, 0))
+                proj_t[h, :, at] = got
+                peak = top[h]
+                for b in range(tile // LANES):
+                    peak = jnp.maximum(peak, jnp.abs(got[:, b * LANES : (b + 1) * LANES]))
+                top[h] = peak
+            return carry
+
+        lax.fori_loop(start, stop, step, 0)
 
     def encode(h):
-        peak = jnp.max(top[...], axis=1, keepdims=True)
+        peak = jnp.max(top[h], axis=1, keepdims=True)
         scale = jnp.maximum(peak, 1e-30) * (1.0 / TOP)
         inv_b[...] = jnp.broadcast_to(1.0 / scale, inv_b.shape)
         flat = jnp.broadcast_to(scale, inv_b.shape)
@@ -174,19 +181,18 @@
 
         def step(t, carry):
             at = pl.ds(pl.multiple_of(t * LANES, LANES), LANES)
-            coded = pack(proj_t[:LANES, at], proj_t[LANES:, at], inv_b[:LANES], inv_b[LANES:])
+            coded = pack(proj_t[h, :LANES, at], proj_t[h, LANES:, at], inv_b[:LANES], inv_b[LANES:])
             packed[at, :] = coded.T
             return carry
 
-        lax.fori_loop(0, nproj // LANES, step, 0)
+        lax.fori_loop(0, nproj // LANES, step, 0, unroll=3)
 
     def gather(dst, h, parity, sub):
         def one(j, carry):
             base = ((j << 1) | parity) * rows + sub * rs
             for g in range(rs // 8):
                 slot = base + 8 * g
-                upper, lower = slot >> 7, slot & 127
-                taken = [packed[pl.ds(inv_s[upper, lower + r], 1), :] for r in range(8)]
+                taken = [packed[pl.ds(inv_s[slot + r], 1), :] for r in range(8)]
                 dst[h, j, pl.ds(sub * rs + 8 * g, 8), :] = jnp.concatenate(taken, axis=0)
             return carry
 
@@ -379,10 +385,10 @@
             permute(stage, lambda p: wave[p], 3 * third, third, 0)
             wave_copy(1, stage).start()
 
-    def build_picked():
+    def build_picked(i):
         @pl.when(k == 0)
         def _():
-            permute(picked, lambda p: wave[p], 0, 3 * third, 0)
+            permute(picked, lambda p: wave[p], i * third, third, i * third)
 
     def add(which, values, fresh):
         for c in range(2):
@@ -559,14 +565,21 @@
         return real, imag
 
     last = streams - 1
+    early = tiles // 3
     invert()
     transpose_waves()
+    top[...] = jnp.zeros_like(top)
+    multiply(range(streams), 0, early)
     pl.semaphore_wait(barrier, len(greet))
     send_waves()
-    small[5].wait()
+    multiply((0,), early, tiles)
     for h in range(streams):
-        multiply(h)
+        if h > 0:
+            multiply((h,), early, tiles)
         encode(h)
+        if h == 0:
+            for copy in inverse_copies:
+                copy.wait()
         for sub in range(parts):
             send_core(h, sub)
         for sub in range(parts):
@@ -577,31 +590,38 @@
     spread_shift()
     if paired:
         send_picked()
-        build_picked()
+        build_picked(0)
+    if paired:
         plane_first(0)
         plane_second(0)
+    step_x(last, 0)
+    if paired:
+        build_picked(1)
         plane_first(1)
-    cosine, sine = make_tables()
-    step_x(last, 0)
+    for sub in range(1, parts):
+        step_x(last, sub)
     for h in range(last):
         for sub in range(parts):
             step_z(h, sub)
-    for sub in range(1, parts):
-        step_x(last, sub)
+    if paired:
+        build_picked(2)
+    cosine, sine = make_tables()
+    for sub in range(parts):
+        step_z(last, sub)
+    for h in range(last):
+        for sub in range(parts):
+            for copy in y_copies(h, sub):
+                copy.wait()
     if paired:
         plane_first(2)
         send_margin(1)
-    for sub in range(parts):
-        step_z(last, sub)
-    if paired:
+        plane_second(1)
         step_margin(1)
-        plane_second(1)
     else:
         plane_ring()
-    for h in range(streams):
-        for sub in range(parts):
-            for copy in y_copies(h, sub):
-                copy.wait()
+    for sub in range(parts):
+        for copy in y_copies(last, sub):
+            copy.wait()
 
     def next_part(take, c):
         lines = []
@@ -624,8 +644,8 @@
         real, imag = finish_margin(1, real, imag)
     real, imag = finish_margin(0, real, imag)
     drain_waves()
-    out[0] = real
-    out[1] = imag
+    out[:, 0, :] = real
+    out[:, 1, :] = imag
 
 
 def fused(n, kn, order, shift, phase, charges, waves, projectors):
@@ -646,10 +666,10 @@
     f32, i32, bf16 = jnp.float32, jnp.int32, jnp.bfloat16
     tile = block_of(nproj) if nproj % 256 else 256
     scratch = [
-        ((1, nproj), i32), ((1, pw_dev), i32), ((1, atoms), f32), ((ppa, pad, atoms), f32),
+        ((nproj // LANES, LANES), i32), ((1, pw_dev), i32), ((1, atoms), f32), ((ppa, pad, atoms), f32),
         ((blocks, LANES), i32), "smem", ((pw_dev, LANES), i32), ((rows, rows), f32),
         ((2, pw_dev, nb), bf16), ((2, pw_dev, nproj), bf16), ((h, 2, 2 * LANES, pw_dev), bf16),
-        ((2 * LANES, nproj), f32), ((2 * LANES, LANES), f32), ((2 * LANES, LANES), f32), ((nproj, LANES), i32),
+        ((h, 2 * LANES, nproj), f32), ((h, 2 * LANES, LANES), f32), ((2 * LANES, LANES), f32), ((nproj, LANES), i32),
         ((h, half, rows, LANES), i32), ((h, half, rows, LANES), i32), ((h, half, rows, LANES), i32),
         ((h, 2, LANES), f32), ((h, 2, LANES), f32),
         ((zn, 2, rows // parts, LANES), f32), ((h, zn, rows, LANES), i32), ((h, zn, rows, LANES), i32),
@@ -663,14 +683,14 @@
         ((kinds, half, share, nb), i32), ((kinds, half, share, nb), i32),
         ((kinds, 2, nb), f32), ((kinds, half, 2, nb), f32),
     ]
-    made = [pltpu.SMEM((blocks, LANES), i32) if s == "smem" else pltpu.VMEM(*s) for s in scratch]
+    made = [pltpu.SMEM((blocks * LANES,), i32) if s == "smem" else pltpu.VMEM(*s) for s in scratch]
     sems = [
-        (nproj // tile + 6,), (2, h, parts), (2, h), (2, h, parts, 2), (2, h, parts, zn - 1, 2),
+        (nproj // tile + 5 + blocks,), (2, h, parts), (2, h), (2, h, parts, 2), (2, h, parts, zn - 1, 2),
         (2, h, parts, 2), (2, slots), (2, kinds, 2), (2, kinds, half, 2),
     ]
     return pl.pallas_call(
         functools.partial(fused_kernel, n, kn, ppa),
-        out_shape=jax.ShapeDtypeStruct((2, share, nb), f32),
+        out_shape=jax.ShapeDtypeStruct((share, 2, nb), f32),
         in_specs=[anywhere] * 6,
         out_specs=pl.BlockSpec(memory_space=pltpu.VMEM),
         scratch_shapes=made + [pltpu.SemaphoreType.DMA(s) for s in sems],
@@ -684,10 +704,10 @@
     n = lax.axis_size("pw")
     kn = lax.axis_size("ka")
     summed = fused(
-        n, kn, projector_order[None, :], shift_map[None, :], atom_phase[None, :],
+        n, kn, projector_order.reshape(-1, LANES), shift_map[None, :], atom_phase[None, :],
         jnp.transpose(charges, (1, 2, 0)), waves, projectors,
     )
-    return jnp.transpose(summed, (1, 0, 2))[None]
+    return summed[None]
 
 
 def solution(mesh):

time: 69.5 us -> 63.6 us (0.915)
  Pallas kernels: 66.5 us -> 62 us
  local copies, waits for them, and re-layouts: 2.71 us -> 1.38 us
    pallas_call x1, Pallas kernels: 66.5 us -> 62 us  [fused(): pl.pallas_call(functools.partial(fused_kernel, n, kn, ppa), out_shape=jax...]
    broadcast_in_dim x2 -> x0, local copies, waits for them, and re-layouts: 2.71 us -> none  [the longest x1 1.4 us: local(): return jnp.transpose(summed, (1, 0, 2))[None]]
    unnamed x0 -> x1, local copies, waits for them, and re-layouts: none -> 1.38 us
where the time goes in v2:
time: 63.6 us; the launch traced here: 63.4 us
  Pallas kernels  62 us (97%)
  local copies, waits for them, and re-layouts  1.38 us (2%)
    pallas_call x1, Pallas kernels, fused(): pl.pallas_call(functools.partial(fused_kernel, n, kn, ppa), out_shape=jax...  62 us
    unnamed x1, local copies, waits for them, and re-layouts  1.38 us

profile of v2, /device:TPU:0, one launch (start us, length us, event | category | flops | bytes accessed | tf_op | source)
XLA Modules:
  0.0 63.4 jit_solution(10761484721730048554)
XLA Ops:
  0.0 62.0 %shard_map.64 = f32[16,2,256]{2,1,0:T(2,128)} custom-call(s32[18,128]{1,0:T(8,128)} %bitcast.7, s32[1,2048]{1,0:T(1,128)} %bitcast.8, f32[1,128]{1,0:T(1,128)} %bitcast.9, f32[18,18,128]{2,1,0:T(8,128)} %bitcast.5, bf16[1,2,2048,256]{3,2,1,0:T(8,128)(2,1)} %wave_hbm.1, bf16[1,2,2048,2304]{3,2,1,0:T(8,128)(2,1)} %beta_hbm.1), custom_call_target="tpu_custom_call" | custom-call | tf_op jit(solution)/shard_map/pallas_call | solution.py:691
  62.1 1.4 %copy.8 = f32[1,16,2,256]{3,2,1,0:T(2,128)} copy(f32[1,16,2,256]{3,2,1,0:T(2,128)} %bitcast.6) | data formatting | bytes 65536

commit v3 on v2

--- a/solution.py
+++ b/solution.py
@@ -1,4 +1,5 @@
 import functools
+import math
 
 import jax
 import jax.numpy as jnp
@@ -62,6 +63,10 @@
         if size % block == 0:
             return block
     return size
+
+
+def pieces_of(rows, ppa):
+    return 2 if rows % 16 == 0 and (rows // 2) % ppa == 0 else 1
 
 
 def fused_kernel(
@@ -80,14 +85,16 @@
     nproj = beta.shape[2]
     streams = nb // LANES
     rows = gs.shape[2]
-    parts = 2 if rows % 16 == 0 else 1
+    parts = pieces_of(rows, ppa)
     rs = rows // parts
     halfn, zn = n // 2, n // 4
     share = nb // n
     core, xbit, mez, mej = me & 1, (me >> 1) & 1, me >> 2, me >> 1
     tile = block_of(nproj) if nproj % 256 else 256
     tiles = nproj // tile
-    third = wr.shape[2]
+    unit = pw_dev // 16
+    cuts = ((0, 4, 8, 11), (0, 5, 10))
+    few = 11 * unit
 
     def beta_copy(t):
         at = pl.ds(pl.multiple_of(t * tile, tile), tile)
@@ -336,25 +343,35 @@
         for copy in y_copies(h, sub):
             copy.start()
 
-    def wave_copy(i, src):
-        return remote(src, wr.at[i], wave_sems.at[0, i], wave_sems.at[1, i], {"ka": behind})
-
-    def own_rows(i):
-        return wave_hbm.at[0, :, pl.ds(i * third, third), :]
+    def wave_copy(i, src, at):
+        return remote(src, wr.at[:, at, :], wave_sems.at[0, i], wave_sems.at[1, i], {"ka": behind})
+
+    def landing(side, i):
+        low_end, high_end = cuts[side][i : i + 2]
+        return pl.ds(low_end * unit, (high_end - low_end) * unit)
+
+    def sent(side, i):
+        if side == 1:
+            return wave_copy(i, wave.at[:, landing(0, i), :], landing(0, i))
+        src = stage if i else wave.at[:, pl.ds(few, pw_dev - few), :]
+        return wave_copy(i, src, landing(1, i))
+
+    def whole_wave():
+        return wave_copy(0, wave, pl.ds(0, pw_dev))
 
     def send_waves():
         if not paired:
-            wave_copy(0, wave_hbm.at[0]).start()
+            whole_wave().start()
             return
 
         @pl.when(k == 0)
         def _():
-            wave_copy(0, own_rows(3)).start()
+            sent(0, 0).start()
 
         @pl.when(k == 1)
         def _():
             for i in range(3):
-                wave_copy(i, own_rows(i)).start()
+                sent(1, i).start()
 
     def spread_shift():
         small[2].wait()
@@ -363,11 +380,11 @@
             spread[pl.ds(b * LANES, LANES), :] = jnp.broadcast_to(line, (LANES, LANES)).T
 
     def permute(dst, src, start, size, offset):
-        block = min(block_of(size), 256)
+        block = next((b for b in (256, 192, 320, 128) if size % b == 0), size)
 
         def step(b, carry):
-            at = pl.ds(pl.multiple_of(start + b * block, block), block)
-            to = pl.ds(pl.multiple_of(offset + b * block, block), block)
+            at = pl.ds(pl.multiple_of(start + b * block, math.gcd(start, block)), block)
+            to = pl.ds(pl.multiple_of(offset + b * block, math.gcd(offset, block)), block)
             want = spread[at, :]
             lane = lax.broadcasted_iota(jnp.int32, (block, LANES), 1)
             hot = jnp.concatenate(
@@ -382,13 +399,14 @@
     def send_picked():
         @pl.when(k == 0)
         def _():
-            permute(stage, lambda p: wave[p], 3 * third, third, 0)
-            wave_copy(1, stage).start()
+            permute(stage, lambda p: wave[p], few, pw_dev - few, 0)
+            sent(0, 1).start()
 
     def build_picked(i):
         @pl.when(k == 0)
         def _():
-            permute(picked, lambda p: wave[p], i * third, third, i * third)
+            start, stop = cuts[0][i] * unit, cuts[0][i + 1] * unit
+            permute(picked, lambda p: wave[p], start, stop - start, start)
 
     def add(which, values, fresh):
         for c in range(2):
@@ -397,52 +415,54 @@
             else:
                 part[which, c] += values[c]
 
-    def piece(ref, i):
-        return [ref[p, i * third : (i + 1) * third, :] for p in range(2)]
+    def piece(ref, start, stop):
+        return [ref[p, start:stop, :] for p in range(2)]
 
     def plane_first(i):
         @pl.when(k == 0)
         def _():
-            wave_copy(i, own_rows(i)).wait_recv()
-            got = [wr[i, 0], wr[i, 1]]
-            add(0, cross(piece(wave, i), got), i == 0)
-            add(1, cross(got, piece(picked, i)), i == 0)
+            sent(1, i).wait_recv()
+            ends = cuts[0][i] * unit, cuts[0][i + 1] * unit
+            got = piece(wr, *ends)
+            add(0, cross(piece(wave, *ends), got), i == 0)
+            add(1, cross(got, piece(picked, *ends)), i == 0)
 
     def plane_second(i):
         @pl.when(k == 1)
         def _():
-            wave_copy(i, own_rows(i)).wait_recv()
-            got = [wr[i, 0], wr[i, 1]]
+            sent(0, i).wait_recv()
+            got = piece(wr, cuts[1][i] * unit, cuts[1][i + 1] * unit)
+            rest = piece(wave, few, pw_dev)
             if i == 0:
-                add(1, cross(got, piece(wave, 3)), True)
+                add(1, cross(got, rest), True)
             else:
-                add(0, cross(piece(wave, 3), got), True)
+                add(0, cross(rest, got), True)
 
     def drain_waves():
         if not paired:
-            wave_copy(0, wave_hbm.at[0]).wait_send()
+            whole_wave().wait_send()
             return
 
         @pl.when(k == 0)
         def _():
-            wave_copy(0, own_rows(3)).wait_send()
-            wave_copy(1, stage).wait_send()
+            for i in range(2):
+                sent(0, i).wait_send()
 
         @pl.when(k == 1)
         def _():
             for i in range(3):
-                wave_copy(i, own_rows(i)).wait_send()
+                sent(1, i).wait_send()
 
     def plane_ring():
-        wave_copy(0, wave_hbm.at[0]).wait_recv()
+        whole_wave().wait_recv()
 
         @pl.when(last_k)
         def _():
-            permute(picked, lambda p: wr[0, p], 0, pw_dev, 0)
+            permute(picked, lambda p: wr[p], 0, pw_dev, 0)
 
         @pl.when(k != kn - 1)
         def _():
-            picked[...] = wr[0]
+            picked[...] = wr[...]
 
         add(0, cross([wave[0], wave[1]], [picked[0], picked[1]]), True)
 
@@ -483,86 +503,102 @@
         sym[...] = jnp.where(same, 0.5 * full, 0.0)
         return cosine, sine
 
-    def m_copies(w):
+    def m_copies(w, h):
         where = {"pw": me ^ 1}
         return [
-            remote(ms.at[w], mr.at[w], m_sems.at[0, w, 0], m_sems.at[1, w, 0], where),
-            remote(scm.at[w], scm_r.at[w], m_sems.at[0, w, 1], m_sems.at[1, w, 1], where),
+            remote(ms.at[w, h], mr.at[w, h], m_sems.at[0, w, h, 0], m_sems.at[1, w, h, 0], where),
+            remote(scm.at[w, h], scm_r.at[w, h], m_sems.at[0, w, h, 1], m_sems.at[1, w, h, 1], where),
         ]
 
-    def d_copies(w):
+    def d_copies(w, h):
         made = []
         for d in range(1 - w, halfn):
             where = {"pw": me ^ (d << 1)}
             if w:
                 where["ka"] = ahead
             made.append(remote(
-                ds.at[w, d], dr.at[w, d], d_sems.at[0, w, d, 0], d_sems.at[1, w, d, 0], where,
+                ds.at[w, h, d], dr.at[w, h, d], d_sems.at[0, w, h, d, 0], d_sems.at[1, w, h, d, 0], where,
             ))
             made.append(remote(
-                scd.at[w], scd_r.at[w, d], d_sems.at[0, w, d, 1], d_sems.at[1, w, d, 1], where,
+                scd.at[w, h], scd_r.at[w, h, d], d_sems.at[0, w, h, d, 1], d_sems.at[1, w, h, d, 1], where,
             ))
         return made
 
-    wide = jnp.zeros((8, nb), jnp.float32)
-
     def block_at(j, parity):
         return pl.ds(pl.multiple_of(((j << 1) | parity) * share, share), share)
 
-    def margin_scale(ref, w, tops):
-        scales = [scale_of(t) for t in tops]
-        ref[w, 0:1, :] = scales[0]
-        ref[w, 1:2, :] = scales[1]
-        return [1.0 / s for s in scales]
-
-    def send_margin(w):
+    def columns(h):
+        return slice(h * LANES, (h + 1) * LANES)
+
+    def send_margin(w, h):
+        cols = columns(h)
+
         def first(j, carry):
             at = block_at(j, 1 - core)
-            return jnp.maximum(carry[0], fold(part[w, 0, at, :])), jnp.maximum(carry[1], fold(part[w, 1, at, :]))
-
-        inv = margin_scale(scm, w, lax.fori_loop(0, halfn, first, (wide, wide)))
+            return (
+                jnp.maximum(carry[0], fold(part[w, 0, at, cols])),
+                jnp.maximum(carry[1], fold(part[w, 1, at, cols])),
+            )
+
+        inv = put_scale(scm, w, h, lax.fori_loop(0, halfn, first, (none, none)))
 
         def second(j, carry):
             at = block_at(j, 1 - core)
-            ms[w, j] = pack(part[w, 0, at, :], part[w, 1, at, :], *inv)
+            ms[w, h, j] = pack(part[w, 0, at, cols], part[w, 1, at, cols], *inv)
             return carry
 
         lax.fori_loop(0, halfn, second, 0)
-        for copy in m_copies(w):
+        for copy in m_copies(w, h):
             copy.start()
 
-    def step_margin(w):
-        for copy in m_copies(w):
+    def step_margin(w, h):
+        for copy in m_copies(w, h):
             copy.wait()
-        s_r, s_i = scm_r[w, 0:1, :], scm_r[w, 1:2, :]
+        cols = columns(h)
+        s_r, s_i = scm_r[w, h, 0:1, :], scm_r[w, h, 1:2, :]
 
         def first(d, carry):
             j = mej ^ d
             at = block_at(j, core)
-            v = mr[w, j]
-            real = part[w, 0, at, :] + low(v) * s_r
-            imag = part[w, 1, at, :] + high(v) * s_i
-            macc[w, d, 0], macc[w, d, 1] = real, imag
+            v = mr[w, h, j]
+            real = part[w, 0, at, cols] + low(v) * s_r
+            imag = part[w, 1, at, cols] + high(v) * s_i
+            macc[w, h, d, 0], macc[w, h, d, 1] = real, imag
             return jnp.maximum(carry[0], fold(real)), jnp.maximum(carry[1], fold(imag))
 
-        inv = margin_scale(scd, w, lax.fori_loop(0, halfn, first, (wide, wide)))
+        inv = put_scale(scd, w, h, lax.fori_loop(0, halfn, first, (none, none)))
 
         def second(d, carry):
-            ds[w, d] = pack(macc[w, d, 0], macc[w, d, 1], *inv)
+            ds[w, h, d] = pack(macc[w, h, d, 0], macc[w, h, d, 1], *inv)
             return carry
 
         lax.fori_loop(1 - w, halfn, second, 0)
-        for copy in d_copies(w):
+        for copy in d_copies(w, h):
             copy.start()
 
-    def finish_margin(w, real, imag):
-        for copy in d_copies(w):
+    def finish_margin(w, h, real, imag):
+        for copy in d_copies(w, h):
             copy.wait()
         for d in range(1 - w, halfn):
-            v = dr[w, d]
-            real = real + low(v) * scd_r[w, d, 0:1, :]
-            imag = imag + high(v) * scd_r[w, d, 1:2, :]
+            v = dr[w, h, d]
+            real = real + low(v) * scd_r[w, h, d, 0:1, :]
+            imag = imag + high(v) * scd_r[w, h, d, 1:2, :]
         return real, imag
+
+    def augment(h, sub, cosine, sine):
+        for copy in y_copies(h, sub):
+            copy.wait()
+        at = slice(sub * rs, (sub + 1) * rs)
+        v = yr[h, at, :]
+        nr, ni = low(v) * scy_r[h, sub, 0:1, :], high(v) * scy_r[h, sub, 1:2, :]
+        c, s = cosine[at], sine[at]
+        turned = jnp.concatenate([nr * c + ni * s, ni * c - nr * s], axis=1)
+        weighted = dot(sym[at, at], turned, (1, 0), HIGH)
+        by_real = contract(mine[0, at, :], weighted, HIGH)
+        by_imag = contract(mine[1, at, :], weighted, HIGH)
+        cols = columns(h)
+        part[0, 0, :, cols] += by_real[:, :LANES] + by_imag[:, LANES:]
+        part[0, 1, :, cols] += by_real[:, LANES:] - by_imag[:, :LANES]
 
     last = streams - 1
     early = tiles // 3
@@ -608,44 +644,36 @@
     cosine, sine = make_tables()
     for sub in range(parts):
         step_z(last, sub)
+    if paired:
+        plane_first(2)
+        plane_second(1)
+    else:
+        plane_ring()
     for h in range(last):
         for sub in range(parts):
-            for copy in y_copies(h, sub):
-                copy.wait()
+            augment(h, sub, cosine, sine)
+        send_margin(0, h)
     if paired:
-        plane_first(2)
-        send_margin(1)
-        plane_second(1)
-        step_margin(1)
-    else:
-        plane_ring()
-    for sub in range(parts):
-        for copy in y_copies(last, sub):
-            copy.wait()
-
-    def next_part(take, c):
-        lines = []
-        for sub in range(parts):
-            pieces = [take(yr[h, span(sub), :]) * scy_r[h, sub, c : c + 1, :] for h in range(streams)]
-            lines.append(jnp.concatenate(pieces, axis=1))
-        return jnp.concatenate(lines, axis=0)
-
-    nr, ni = next_part(low, 0), next_part(high, 1)
-    turned = jnp.concatenate([nr * cosine + ni * sine, ni * cosine - nr * sine], axis=1)
-    weighted = dot(sym[...], turned, (1, 0), HIGH)
-    by_real = contract(mine[0], weighted, HIGH)
-    by_imag = contract(mine[1], weighted, HIGH)
-    part[0, 0] += by_real[:, :nb] + by_imag[:, nb:]
-    part[0, 1] += by_real[:, nb:] - by_imag[:, :nb]
-    send_margin(0)
-    step_margin(0)
-    real, imag = macc[0, 0, 0], macc[0, 0, 1]
+        for h in range(streams):
+            send_margin(1, h)
+    for h in range(last):
+        step_margin(0, h)
+    for sub in range(parts - 1):
+        augment(last, sub, cosine, sine)
     if paired:
-        real, imag = finish_margin(1, real, imag)
-    real, imag = finish_margin(0, real, imag)
+        for h in range(streams):
+            step_margin(1, h)
+    augment(last, parts - 1, cosine, sine)
+    send_margin(0, last)
+    step_margin(0, last)
     drain_waves()
-    out[:, 0, :] = real
-    out[:, 1, :] = imag
+    for h in range(streams):
+        real, imag = macc[0, h, 0, 0], macc[0, h, 0, 1]
+        if paired:
+            real, imag = finish_margin(1, h, real, imag)
+        real, imag = finish_margin(0, h, real, imag)
+        out[:, 0, columns(h)] = real
+        out[:, 1, columns(h)] = imag
 
 
 def fused(n, kn, order, shift, phase, charges, waves, projectors):
@@ -655,12 +683,14 @@
     ppa = charges.shape[0]
     rows, share = nproj // n, nb // n
     h = nb // LANES
-    parts = 2 if rows % 16 == 0 else 1
+    parts = pieces_of(rows, ppa)
     zn, half = n // 4, n // 2
     pad = -(-ppa // 8) * 8
     blocks = -(-nproj // (8 * LANES)) * 8
     paired = kn == 2
-    slots, third = (3, pw_dev // 4) if paired else (1, pw_dev)
+    unit = pw_dev // 16
+    sent_rows = 11 * unit if paired else pw_dev
+    slots = 3 if paired else 1
     kinds = 2 if paired else 1
     anywhere = pl.BlockSpec(memory_space=pl.ANY)
     f32, i32, bf16 = jnp.float32, jnp.int32, jnp.bfloat16
@@ -677,20 +707,20 @@
         ((h, zn - 1, rows, LANES), i32), ((h, zn - 1, rows, LANES), i32),
         ((h, parts, 2, LANES), f32), ((h, parts, zn - 1, 2, LANES), f32), ((2, rows, nb), f32),
         ((h, rows, LANES), i32), ((h, rows, LANES), i32), ((h, parts, 2, LANES), f32), ((h, parts, 2, LANES), f32),
-        ((slots, 2, third, nb), bf16), ((2, slots * third, nb), bf16), ((2, third, nb), bf16),
-        ((kinds, 2, nb, nb), f32), ((kinds, half, share, nb), i32), ((kinds, half, share, nb), i32),
-        ((kinds, 2, nb), f32), ((kinds, 2, nb), f32), ((kinds, half, 2, share, nb), f32),
-        ((kinds, half, share, nb), i32), ((kinds, half, share, nb), i32),
-        ((kinds, 2, nb), f32), ((kinds, half, 2, nb), f32),
+        ((2, sent_rows, nb), bf16), ((2, sent_rows, nb), bf16), ((2, 5 * unit, nb), bf16),
+        ((kinds, 2, nb, nb), f32), ((kinds, h, half, share, LANES), i32), ((kinds, h, half, share, LANES), i32),
+        ((kinds, h, 2, LANES), f32), ((kinds, h, 2, LANES), f32), ((kinds, h, half, 2, share, LANES), f32),
+        ((kinds, h, half, share, LANES), i32), ((kinds, h, half, share, LANES), i32),
+        ((kinds, h, 2, LANES), f32), ((kinds, h, half, 2, LANES), f32),
     ]
     made = [pltpu.SMEM((blocks * LANES,), i32) if s == "smem" else pltpu.VMEM(*s) for s in scratch]
     sems = [
         (nproj // tile + 5 + blocks,), (2, h, parts), (2, h), (2, h, parts, 2), (2, h, parts, zn - 1, 2),
-        (2, h, parts, 2), (2, slots), (2, kinds, 2), (2, kinds, half, 2),
+        (2, h, parts, 2), (2, slots), (2, kinds, h, 2), (2, kinds, h, half, 2),
     ]
     return pl.pallas_call(
         functools.partial(fused_kernel, n, kn, ppa),
-        out_shape=jax.ShapeDtypeStruct((share, 2, nb), f32),
+        out_shape=pltpu.VMEM((share, 2, nb), f32),
         in_specs=[anywhere] * 6,
         out_specs=pl.BlockSpec(memory_space=pltpu.VMEM),
         scratch_shapes=made + [pltpu.SemaphoreType.DMA(s) for s in sems],

time: 63.6 us -> 61.2 us (0.962)
  Pallas kernels: 62 us -> 60.3 us
  local copies, waits for them, and re-layouts: 1.38 us -> 0.62 us
    pallas_call x1, Pallas kernels: 62 us -> 60.3 us  [fused(): pl.pallas_call(functools.partial(fused_kernel, n, kn, ppa), out_shape=plt...]
    unnamed x1, local copies, waits for them, and re-layouts: 1.38 us -> 0.62 us
where the time goes in v3:
time: 61.2 us; the launch traced here: 61 us
  Pallas kernels  60.3 us (99%)
  local copies, waits for them, and re-layouts  0.62 us (1%)
    pallas_call x1, Pallas kernels, fused(): pl.pallas_call(functools.partial(fused_kernel, n, kn, ppa), out_shape=plt...  60.3 us

profile of v3, /device:TPU:0, one launch (start us, length us, event | category | flops | bytes accessed | tf_op | source)
XLA Modules:
  0.0 61.0 jit_solution(9133409385520886108)
XLA Ops:
  0.0 60.3 %shard_map.64 = f32[16,2,256]{2,1,0:T(2,128)S(1)} custom-call(s32[18,128]{1,0:T(8,128)} %bitcast.7, s32[1,2048]{1,0:T(1,128)} %bitcast.8, f32[1,128]{1,0:T(1,128)} %bitcast.9, f32[18,18,128]{2,1,0:T(8,128)} %bitcast.6, bf16[1,2,2048,256]{3,2,1,0:T(8,128)(2,1)} %wave_hbm.1, bf16[1,2,2048,2304]{3,2,1,0:T(8,128)(2,1)} %beta_hbm.1), custom_call_target="tpu_custom_call" | custom-call | tf_op jit(solution)/shard_map/pallas_call | solution.py:721
  60.3 0.6 %copy.8 = f32[1,16,2,256]{3,2,1,0:T(2,128)} copy(f32[1,16,2,256]{3,2,1,0:T(2,128)S(1)} %bitcast.5) | data formatting | bytes 65536

commit v4 on v3

--- a/solution.py
+++ b/solution.py
@@ -92,9 +92,9 @@
     core, xbit, mez, mej = me & 1, (me >> 1) & 1, me >> 2, me >> 1
     tile = block_of(nproj) if nproj % 256 else 256
     tiles = nproj // tile
-    unit = pw_dev // 16
-    cuts = ((0, 4, 8, 11), (0, 5, 10))
-    few = 11 * unit
+    unit = pw_dev // 32
+    cuts = ((0, 8, 16, 21), (0, 11, 22))
+    few = 21 * unit
 
     def beta_copy(t):
         at = pl.ds(pl.multiple_of(t * tile, tile), tile)
@@ -380,7 +380,7 @@
             spread[pl.ds(b * LANES, LANES), :] = jnp.broadcast_to(line, (LANES, LANES)).T
 
     def permute(dst, src, start, size, offset):
-        block = next((b for b in (256, 192, 320, 128) if size % b == 0), size)
+        block = next((b for b in (256, 192, 320, 352, 128) if size % b == 0), size)
 
         def step(b, carry):
             at = pl.ds(pl.multiple_of(start + b * block, math.gcd(start, block)), block)
@@ -586,8 +586,9 @@
         return real, imag
 
     def augment(h, sub, cosine, sine):
-        for copy in y_copies(h, sub):
-            copy.wait()
+        if not paired or h + sub > 0:
+            for copy in y_copies(h, sub):
+                copy.wait()
         at = slice(sub * rs, (sub + 1) * rs)
         v = yr[h, at, :]
         nr, ni = low(v) * scy_r[h, sub, 0:1, :], high(v) * scy_r[h, sub, 1:2, :]
@@ -610,6 +611,10 @@
     send_waves()
     multiply((0,), early, tiles)
     for h in range(streams):
+        if h == last:
+            spread_shift()
+            if paired:
+                send_picked()
         if h > 0:
             multiply((h,), early, tiles)
         encode(h)
@@ -623,29 +628,34 @@
             step_core(h, sub)
             if h > 0:
                 step_x(h - 1, sub)
-    spread_shift()
+    step_x(last, 0)
     if paired:
-        send_picked()
         build_picked(0)
-    if paired:
         plane_first(0)
         plane_second(0)
-    step_x(last, 0)
+    for sub in range(1, parts):
+        step_x(last, sub)
     if paired:
         build_picked(1)
         plane_first(1)
-    for sub in range(1, parts):
-        step_x(last, sub)
     for h in range(last):
         for sub in range(parts):
             step_z(h, sub)
     if paired:
         build_picked(2)
     cosine, sine = make_tables()
-    for sub in range(parts):
+    for sub in range(parts - 1):
         step_z(last, sub)
     if paired:
         plane_first(2)
+        for h in range(streams):
+            send_margin(1, h)
+    step_z(last, parts - 1)
+    if paired:
+        for copy in y_copies(0, 0):
+            copy.wait()
+        for h in range(streams):
+            step_margin(1, h)
         plane_second(1)
     else:
         plane_ring()
@@ -653,16 +663,10 @@
         for sub in range(parts):
             augment(h, sub, cosine, sine)
         send_margin(0, h)
-    if paired:
-        for h in range(streams):
-            send_margin(1, h)
+    for sub in range(parts - 1):
+        augment(last, sub, cosine, sine)
     for h in range(last):
         step_margin(0, h)
-    for sub in range(parts - 1):
-        augment(last, sub, cosine, sine)
-    if paired:
-        for h in range(streams):
-            step_margin(1, h)
     augment(last, parts - 1, cosine, sine)
     send_margin(0, last)
     step_margin(0, last)
@@ -688,8 +692,8 @@
     pad = -(-ppa // 8) * 8
     blocks = -(-nproj // (8 * LANES)) * 8
     paired = kn == 2
-    unit = pw_dev // 16
-    sent_rows = 11 * unit if paired else pw_dev
+    unit = pw_dev // 32
+    sent_rows = 22 * unit if paired else pw_dev
     slots = 3 if paired else 1
     kinds = 2 if paired else 1
     anywhere = pl.BlockSpec(memory_space=pl.ANY)
@@ -707,7 +711,7 @@
         ((h, zn - 1, rows, LANES), i32), ((h, zn - 1, rows, LANES), i32),
         ((h, parts, 2, LANES), f32), ((h, parts, zn - 1, 2, LANES), f32), ((2, rows, nb), f32),
         ((h, rows, LANES), i32), ((h, rows, LANES), i32), ((h, parts, 2, LANES), f32), ((h, parts, 2, LANES), f32),
-        ((2, sent_rows, nb), bf16), ((2, sent_rows, nb), bf16), ((2, 5 * unit, nb), bf16),
+        ((2, sent_rows, nb), bf16), ((2, sent_rows, nb), bf16), ((2, 11 * unit, nb), bf16),
         ((kinds, 2, nb, nb), f32), ((kinds, h, half, share, LANES), i32), ((kinds, h, half, share, LANES), i32),
         ((kinds, h, 2, LANES), f32), ((kinds, h, 2, LANES), f32), ((kinds, h, half, 2, share, LANES), f32),
         ((kinds, h, half, share, LANES), i32), ((kinds, h, half, share, LANES), i32),

time: 61.2 us -> 58.6 us (0.958)
  Pallas kernels: 60.3 us -> 57.8 us
    pallas_call x1, Pallas kernels: 60.3 us -> 57.8 us  [fused(): pl.pallas_call(functools.partial(fused_kernel, n, kn, ppa), out_shape=plt...]
where the time goes in v4:
time: 58.6 us; the launch traced here: 58.4 us
  Pallas kernels  57.8 us (99%)
  local copies, waits for them, and re-layouts  0.62 us (1%)
    pallas_call x1, Pallas kernels, fused(): pl.pallas_call(functools.partial(fused_kernel, n, kn, ppa), out_shape=plt...  57.8 us

profile of v4, /device:TPU:0, one launch (start us, length us, event | category | flops | bytes accessed | tf_op | source)
XLA Modules:
  0.0 58.4 jit_solution(1952936896658626116)
XLA Ops:
  0.0 57.8 %shard_map.64 = f32[16,2,256]{2,1,0:T(2,128)S(1)} custom-call(s32[18,128]{1,0:T(8,128)} %bitcast.7, s32[1,2048]{1,0:T(1,128)} %bitcast.8, f32[1,128]{1,0:T(1,128)} %bitcast.9, f32[18,18,128]{2,1,0:T(8,128)} %bitcast.6, bf16[1,2,2048,256]{3,2,1,0:T(8,128)(2,1)} %wave_hbm.1, bf16[1,2,2048,2304]{3,2,1,0:T(8,128)(2,1)} %beta_hbm.1), custom_call_target="tpu_custom_call" | custom-call | tf_op jit(solution)/shard_map/pallas_call | solution.py:725
  57.8 0.6 %copy.8 = f32[1,16,2,256]{3,2,1,0:T(2,128)} copy(f32[1,16,2,256]{3,2,1,0:T(2,128)S(1)} %bitcast.5) | data formatting | bytes 65536

commit v5 on v4

--- a/solution.py
+++ b/solution.py
@@ -612,7 +612,8 @@
     multiply((0,), early, tiles)
     for h in range(streams):
         if h == last:
-            spread_shift()
+            if streams == 1:
+                spread_shift()
             if paired:
                 send_picked()
         if h > 0:
@@ -625,6 +626,8 @@
             send_core(h, sub)
         for sub in range(parts):
             gather(go, h, core, sub)
+            if h + sub == 0 and streams > 1:
+                spread_shift()
             step_core(h, sub)
             if h > 0:
                 step_x(h - 1, sub)

time: 58.6 us -> 58.6 us (level)
  no operation moved by 1% of the time
where the time goes in v5:
time: 58.6 us; the launch traced here: 58.4 us
  Pallas kernels  57.8 us (99%)
  local copies, waits for them, and re-layouts  0.62 us (1%)
    pallas_call x1, Pallas kernels, fused(): pl.pallas_call(functools.partial(fused_kernel, n, kn, ppa), out_shape=plt...  57.8 us

profile of v5, /device:TPU:0, one launch (start us, length us, event | category | flops | bytes accessed | tf_op | source)
XLA Modules:
  0.0 58.4 jit_solution(16005261570851826812)
XLA Ops:
  0.0 57.8 %shard_map.64 = f32[16,2,256]{2,1,0:T(2,128)S(1)} custom-call(s32[18,128]{1,0:T(8,128)} %bitcast.7, s32[1,2048]{1,0:T(1,128)} %bitcast.8, f32[1,128]{1,0:T(1,128)} %bitcast.9, f32[18,18,128]{2,1,0:T(8,128)} %bitcast.6, bf16[1,2,2048,256]{3,2,1,0:T(8,128)(2,1)} %wave_hbm.1, bf16[1,2,2048,2304]{3,2,1,0:T(8,128)(2,1)} %beta_hbm.1), custom_call_target="tpu_custom_call" | custom-call | tf_op jit(solution)/shard_map/pallas_call | solution.py:728
  57.8 0.6 %copy.8 = f32[1,16,2,256]{3,2,1,0:T(2,128)} copy(f32[1,16,2,256]{3,2,1,0:T(2,128)S(1)} %bitcast.5) | data formatting | bytes 65536
